TPU v7x, 16 devices: a 4x2x1 block of a 4x4x8 slice. The times are simulated.
16 devices in a mesh: dp: 2 (over y, z), ep: 8 (over x, core).
Axes of the slice: x: 4, y: 2, z: 1, core: 2. Of those that a mesh axis runs over, the one named last changes fastest.
The devices are a block of a 4x4x8 slice.
Arguments:
- h0: bfloat16 [16, 1024, 2048], P(('dp', 'ep')), parts along dimension 0
- idx: int32 [16, 1024, 6], P(('dp', 'ep')), parts along dimension 0
- slot: int32 [16, 1024, 6], P(('dp', 'ep')), parts along dimension 0
- ln_attn: bfloat16 [2048], replicated
- wq: bfloat16 [2048, 2048], replicated
- wk: bfloat16 [2048, 2048], replicated
- wv: bfloat16 [2048, 2048], replicated
- wo: bfloat16 [2048, 2048], replicated
- ln_ffn: bfloat16 [2048], replicated
- ws1: bfloat16 [2048, 2816], replicated
- ws3: bfloat16 [2048, 2816], replicated
- ws2: bfloat16 [2816, 2048], replicated
- ln_moe: bfloat16 [2048], replicated
- wr: bfloat16 [2048, 64], replicated
- ue1: bfloat16 [64, 2048, 1408], P('ep')
- ue3: bfloat16 [64, 2048, 1408], P('ep')
- ue2: bfloat16 [64, 1408, 2048], P('ep')
Outputs:
- output: bfloat16 [16, 1024, 2048], P(('dp', 'ep')), parts along dimension 0
There are 2 independent parts. A program takes and returns all parts, laid end to end along the dimension named above; an argument that names none is the same for every part.
All inputs are finite; a program needn't handle non-finite values.
Results may differ from a plain program's by a relative error of at most 0.0102599.
Values are sent between devices in bfloat16 or wider.
A program may use at most 768 MiB of HBM per device.

v0:
```python
import jax
import jax.numpy as jnp
from jax import lax
from jax.sharding import PartitionSpec as P

HEAD = 128
EPS = 1e-6
CAP_FACTOR = 2


def _mm(form, a, b):
    return jnp.einsum(form, a, b, preferred_element_type=jnp.float32)


def _rms(x, w):
    xf = x.astype(jnp.float32)
    r = lax.rsqrt(jnp.mean(xf * xf, axis=-1, keepdims=True) + EPS)
    return (xf * r * w.astype(jnp.float32)).astype(jnp.bfloat16)


def _rope(x):
    s, half = x.shape[1], x.shape[-1] // 2
    freq = 10000.0 ** (-jnp.arange(half, dtype=jnp.float32) / half)
    ang = jnp.arange(s, dtype=jnp.float32)[:, None] * freq[None, :]
    c = jnp.cos(ang)[None, :, None, :]
    sn = jnp.sin(ang)[None, :, None, :]
    x1, x2 = x[..., :half], x[..., half:]
    return jnp.concatenate([x1 * c - x2 * sn, x2 * c + x1 * sn], axis=-1)


def _dense(h0, ln_attn, wq, wk, wv, wo, ln_ffn, ws1, ws3, ws2):
    b, s, _ = h0.shape
    nh = wq.shape[1] // HEAD
    x1 = _rms(h0, ln_attn)
    q = _rope(_mm('bsd,de->bse', x1, wq).reshape(b, s, nh, HEAD)).astype(jnp.bfloat16)
    k = _rope(_mm('bsd,de->bse', x1, wk).reshape(b, s, nh, HEAD)).astype(jnp.bfloat16)
    v = _mm('bsd,de->bse', x1, wv).astype(jnp.bfloat16).reshape(b, s, nh, HEAD)
    sc = _mm('bqhe,bkhe->bhqk', q, k) * HEAD ** -0.5
    causal = jnp.arange(s)[:, None] >= jnp.arange(s)[None, :]
    p = jax.nn.softmax(jnp.where(causal, sc, -1e30), axis=-1).astype(jnp.bfloat16)
    o = _mm('bhqk,bkhe->bqhe', p, v).astype(jnp.bfloat16).reshape(b, s, nh * HEAD)
    a = (h0.astype(jnp.float32) + _mm('bse,ed->bsd', o, wo)).astype(jnp.bfloat16)
    x2 = _rms(a, ln_ffn)
    hs = (jax.nn.silu(_mm('bsd,df->bsf', x2, ws1)) * _mm('bsd,df->bsf', x2, ws3)).astype(jnp.bfloat16)
    return a, _mm('bsf,fd->bsd', hs, ws2)


def _experts(x, ue1, ue3, ue2):
    he = (jax.nn.silu(_mm('gecd,edf->egcf', x, ue1)) * _mm('gecd,edf->egcf', x, ue3)).astype(jnp.bfloat16)
    return _mm('egcf,efd->gecd', he, ue2).astype(jnp.bfloat16)


def _gate(u, wr, gi):
    lg = _mm('td,de->te', u, wr)
    hit = gi[..., None] == jnp.arange(wr.shape[1], dtype=gi.dtype)
    return jax.nn.softmax(jnp.sum(jnp.where(hit, lg[:, None, :], 0.0), axis=-1), axis=-1)


def _route(q, gate, n):
    hit = q[..., None] == jnp.arange(n, dtype=q.dtype)
    disp = jnp.any(hit, axis=-2).astype(jnp.bfloat16)
    comb = jnp.sum(jnp.where(hit, gate[..., None], 0.0), axis=-2)
    return disp, comb


def _parts(c):
    hi = c.astype(jnp.bfloat16)
    r = c - hi.astype(jnp.float32)
    mid = r.astype(jnp.bfloat16)
    lo = (r - mid.astype(jnp.float32)).astype(jnp.bfloat16)
    return hi, mid, lo


def solution(mesh):
    g_ = mesh.shape['ep']
    rows = P(('dp', 'ep'))
    rep = P()

    def local(h0, idx, slot, ln_attn, wq, wk, wv, wo, ln_ffn, ws1, ws3, ws2, ln_moe, wr, ue1, ue3, ue2):
        b, s, d = h0.shape
        top = idx.shape[-1]
        el = ue1.shape[0]
        ne = el * g_
        t = b * s
        cap = CAP_FACTOR * t * top // ne
        a, fo = _dense(h0, ln_attn, wq, wk, wv, wo, ln_ffn, ws1, ws3, ws2)
        u = _rms(h0, ln_moe).reshape(t, d)
        gi = idx.reshape(t, top)
        sl = slot.reshape(t, top)
        gate = _gate(u, wr, gi)
        disp, comb = _route(gi * cap + sl, gate, ne * cap)
        send = _mm('tr,td->rd', disp, u).astype(jnp.bfloat16).reshape(g_, el, cap, d)
        recv = lax.all_to_all(send, 'ep', 0, 0, tiled=True)
        y = _experts(recv, ue1, ue3, ue2)
        back = lax.all_to_all(y, 'ep', 0, 0, tiled=True).reshape(ne * cap, d)
        m = sum(_mm('tr,rd->td', p, back) for p in _parts(comb))
        out = a.astype(jnp.float32) + fo + m.reshape(b, s, d)
        return out.astype(jnp.bfloat16)

    specs = (rows, rows, rows) + (rep,) * 11 + (P('ep'), P('ep'), P('ep'))
    return jax.shard_map(local, mesh=mesh, in_specs=specs, out_specs=rows, check_vma=False)
```

profile of v0, /device:TPU:112, one launch (start us, length us, event | category | flops | bytes accessed | tf_op | source)
XLA Modules:
  0.0 1763.2 jit_solution(14552785561758742807)
XLA Ops:
  0.0 3.1 fusion.26
  3.2 0.8 bitcast_add_fusion
  4.5 64.1 %fusion.1 = pred[1024,12288]{1,0:T(32,128)(4,1)} fusion(s32[1024,6]{0,1:T(8,128)S(1)} %bitcast_add_fusion), kind=kLoop, calls=%fused_computation.3 | loop fusion | flops 138412032 | bytes 12607488 | tf_op jit(solution)/shard_map/reduce_or | solution.py:61
  68.7 62.1 %convolution_convert_fusion = bf16[12288,2048]{1,0:T(8,128)(2,1)} fusion(pred[1024,12288]{1,0:T(32,128)(4,1)} %fusion.1, bf16[1,1024,2048]{2,1,0:T(8,128)(2,1)} %param.17, f32[2048]{0:T(1024)S(1)} %convert_element_type.103, f32[1024]{0:T(1024)S(1)} %add_rsqrt_fusion.1), kind=kOutput, calls=%fused_computation.17 | convolution fusion | flops 51573161984 | bytes 67121152 | tf_op jit(solution)/shard_map/tr,td->rd/dot_general | solution.py:12
  130.8 559.2 %all_to_all.10 = bf16[8,8,192,2048]{3,2,1,0:T(8,128)(2,1)} all-to-all(bf16[8,8,192,2048]{3,2,1,0:T(8,128)(2,1)} %bitcast.100), channel_id=1, replica_groups=mesh['dp'=2,'ep'=8] {'ep'}, dimensions={0} | all-to-all | bytes 100663296 | tf_op jit(solution)/shard_map/all_to_all | solution.py:93
  690.0 87.8 %fusion.5 = f32[8,8,192,1408]{3,2,1,0:T(8,128)} fusion(bf16[8,2048,1408]{2,1,0:T(8,128)(2,1)} %param.32, bf16[8,8,192,2048]{3,2,1,0:T(8,128)(2,1)} %all_to_all.10), kind=kOutput, calls=%fused_computation.14 | convolution fusion | flops 70866960384 | bytes 165675008 | tf_op jit(solution)/shard_map/gecd,edf->egcf/dot_general | solution.py:12
  777.8 98.4 %multiply_convert_fusion = bf16[8,8,192,1408]{3,2,1,0:T(8,128)(2,1)} fusion(f32[8,8,192,1408]{3,2,1,0:T(8,128)} %fusion.5, bf16[8,2048,1408]{2,1,0:T(8,128)(2,1)} %param.31, bf16[8,8,192,2048]{3,2,1,0:T(8,128)(2,1)} %all_to_all.10), kind=kOutput, calls=%fused_computation.4 | convolution fusion | flops 70970769408 | bytes 200278016 | tf_op jit(solution)/shard_map/gecd,edf->egcf/dot_general | solution.py:12
  876.1 87.9 %convert_bitcast_fusion = bf16[8,8,192,2048]{3,2,0,1:T(8,128)(2,1)} fusion(bf16[8,8,192,1408]{3,2,1,0:T(8,128)(2,1)} %multiply_convert_fusion, bf16[8,1408,2048]{2,1,0:T(8,128)(2,1)} %param.33), kind=kOutput, calls=%fused_computation.11 | convolution fusion | flops 70892126208 | bytes 131072000 | tf_op jit(solution)/shard_map/egcf,efd->gecd/dot_general | solution.py:12
  964.1 33.4 %copy.59 = bf16[8,8,192,2048]{3,2,1,0:T(8,128)(2,1)} copy(bf16[8,8,192,2048]{3,2,0,1:T(8,128)(2,1)} %convert_bitcast_fusion) | data formatting | bytes 100663296 | tf_op jit(solution)/shard_map/convert_element_type | solution.py:50
  997.5 9.1 all-to-all-start.1
  1006.7 13.9 fusion.43
  1020.6 6.4 copy.66
  1027.0 12.4 copy.67
  1039.4 12.3 copy.68
  1052.2 3.6 fusion.62
  1056.8 1.3 iota_compare_fusion.1
  1058.1 1.0 fusion.65
  1059.1 12.9 fusion.46
  1072.0 16.1 fusion.49
  1088.0 4.7 fusion.54
  1092.7 37.2 %fusion.77 = (f32[16,1024]{1,0:T(8,128)S(1)}, f32[16,1024,1024]{1,2,0:T(8,128)}) fusion(pred[1024,1024]{0,1:T(8,128)(4,1)} %iota_compare_fusion.1, bf16[1024,16,64]{0,2,1:T(8,128)(2,1)} %get-tuple-element.9, bf16[1024,16,64]{0,2,1:T(8,128)(2,1)} %get-tuple-element.10, bf16[1024,16,64]{0,2,1:T(8,128)(2,1)} %get-tuple-element.6, ...), kind=kOutput, calls=%fused_computation.91 | convolution fusion | flops 4378854400 | bytes 76611584 | tf_op jit(solution)/shard_map/sub | solution.py:40
  1129.9 25.1 %fusion.53 = bf16[16,128,1024]{2,1,0:T(8,128)(2,1)} fusion(bf16[1024,16,128]{0,2,1:T(8,128)(2,1)} %bitcast.107, f32[16,1024,1024]{1,2,0:T(8,128)} %get-tuple-element.14, f32[16,1024]{1,0:T(8,128)S(1)} %get-tuple-element.13), kind=kOutput, calls=%fused_computation.67 | convolution fusion | flops 4330618880 | bytes 75563008 | tf_op jit(solution)/shard_map/bhqk,bkhe->bqhe/dot_general | solution.py:12
  1155.1 14.1 fusion.28
  1169.3 1.9 copy-done.18
  1171.3 17.9 %fusion.59 = f32[1024,2816]{1,0:T(8,128)} fusion(bf16[2048,2816]{1,0:T(8,128)(2,1)} %param.26, bf16[1,1024,2048]{2,1,0:T(8,128)(2,1)S(1)} %get-tuple-element.16, f32[2048]{0:T(1024)S(1)} %copy-done.10, f32[1024]{0:T(1024)S(1)} %add_rsqrt_fusion), kind=kOutput, calls=%fused_computation.74 | convolution fusion | flops 11819548672 | bytes 27275264 | tf_op jit(solution)/shard_map/bsd,df->bsf/dot_general | solution.py:12
  1189.2 17.6 %multiply_convert_fusion.1 = bf16[1024,2816]{1,0:T(8,128)(2,1)} fusion(f32[1024,2816]{1,0:T(8,128)} %fusion.59, bf16[2048,2816]{1,0:T(8,128)(2,1)S(1)} %bitcast.110, bf16[1,1024,2048]{2,1,0:T(8,128)(2,1)} %copy-done.18, f32[2048]{0:T(1024)S(1)} %copy-done.10, f32[1024]{0:T(1024)S(1)} %add_rsqrt_fusion), kind=kOutput, calls=%fused_computation.35 | convolution fusion | flops 11836850176 | bytes 33042432 | tf_op jit(solution)/shard_map/bsd,df->bsf/dot_general | solution.py:12
  1206.9 58.1 %select_reduce_fusion = f32[1024,12288]{1,0:T(8,128)} fusion(f32[1024,6]{0,1:T(8,128)S(1)} %fusion.66, s32[1024,6]{0,1:T(8,128)S(1)} %copy-done.5), kind=kLoop, calls=%fused_computation.1 | loop fusion | flops 213909504 | bytes 50380800 | tf_op jit(solution)/shard_map/reduce_sum | solution.py:62
  1264.9 285.5 %all-to-all-done.1 = bf16[8,8,192,2048]{3,2,1,0:T(8,128)(2,1)} async-done(((bf16[8,8,192,2048]{3,2,1,0:T(8,128)(2,1)}), bf16[8,8,192,2048]{3,2,1,0:T(8,128)(2,1)}, u32[]{:S(2)}, u32[]{:S(2)}) %all-to-all-start.1) | async-done | bytes 50331680 | tf_op jit(solution)/shard_map/all_to_all | solution.py:95
  1550.4 63.1 %fusion.21 = f32[1024,2048]{1,0:T(8,128)} fusion(bf16[12288,2048]{1,0:T(8,128)(2,1)} %bitcast.28, f32[1024,12288]{1,0:T(8,128)} %select_reduce_fusion), kind=kOutput, calls=%fused_computation.28 | convolution fusion | flops 51627687936 | bytes 109051904 | tf_op jit(solution)/shard_map/tr,rd->td/dot_general | solution.py:12
  1613.6 61.6 %fusion.11 = f32[1024,2048]{1,0:T(8,128)} fusion(bf16[12288,2048]{1,0:T(8,128)(2,1)} %bitcast.28, f32[1024,12288]{1,0:T(8,128)} %select_reduce_fusion), kind=kOutput, calls=%fused_computation.21 | convolution fusion | flops 51552190464 | bytes 109051904 | tf_op jit(solution)/shard_map/tr,rd->td/dot_general | solution.py:12
  1675.1 63.2 %fusion.13 = f32[1024,2048]{1,0:T(8,128)} fusion(bf16[12288,2048]{1,0:T(8,128)(2,1)} %bitcast.28, f32[1024,12288]{1,0:T(8,128)} %select_reduce_fusion), kind=kOutput, calls=%fused_computation.23 | convolution fusion | flops 51589939200 | bytes 109051904 | tf_op jit(solution)/shard_map/tr,rd->td/dot_general | solution.py:12
  1738.3 24.4 %fusion.32 = bf16[1,1024,2048]{2,1,0:T(8,128)(2,1)} fusion(bf16[1,1024,2048]{2,1,0:T(8,128)(2,1)} %copy-done.18, f32[1024,2048]{1,0:T(8,128)} %fusion.21, f32[1024,2048]{1,0:T(8,128)} %fusion.11, f32[1024,2048]{1,0:T(8,128)} %fusion.13, bf16[1024,2816]{1,0:T(8,128)(2,1)} %multiply_convert_fusion.1, bf16[2816,2048]{1,0:T(8,128)(2,1)} %param.28), kind=kOutput, calls=%fused_computation.46 | convolution fusion | flops 11823742976 | bytes 50855936 | tf_op jit(solution)/shard_map/bsf,fd->bsd/dot_general | solution.py:12
  (60 shorter events, 2.2 us)
Async XLA Ops:
  0.0 1052.2 %copy-start = (bf16[2048,64]{0,1:T(8,128)(2,1)S(1)}, bf16[2048,64]{0,1:T(8,128)(2,1)}, u32[]{:S(2)}) copy-start(bf16[2048,64]{0,1:T(8,128)(2,1)} %param.30) | copy-start | bytes 786436
  0.0 68.7 %copy-start.13 = (bf16[2048]{0:T(1024)(128)(2,1)S(1)}, bf16[2048]{0:T(1024)(128)(2,1)}, u32[]{:S(2)}) copy-start(bf16[2048]{0:T(1024)(128)(2,1)} %param.29) | copy-start | bytes 12292
  3.1 127.7 %copy-start.16 = (f32[1024]{0:T(1024)}, f32[1024]{0:T(1024)S(1)}, u32[]{:S(2)}) copy-start(f32[1024]{0:T(1024)S(1)} %add_rsqrt_fusion.1) | copy-start | bytes 12292
  3.9 0.6 copy-start.4
  68.7 62.1 %copy-start.11 = (f32[2048]{0:T(1024)}, f32[2048]{0:T(1024)S(1)}, u32[]{:S(2)}) copy-start(f32[2048]{0:T(1024)S(1)} %convert_element_type.103) | copy-start | bytes 24580
  997.5 9.1 copy-start.6
  997.5 9.2 copy-start.14
  997.5 9.2 copy-start.17
  997.5 552.9 %all-to-all-start.1 = ((bf16[8,8,192,2048]{3,2,1,0:T(8,128)(2,1)}), bf16[8,8,192,2048]{3,2,1,0:T(8,128)(2,1)}, u32[]{:S(2)}, u32[]{:S(2)}) async-start(bf16[8,8,192,2048]{3,2,1,0:T(8,128)(2,1)} %copy.59), calls=%async_computation.1 | async-start | bytes 100663296 | tf_op jit(solution)/shard_map/all_to_all | solution.py:95
  1039.4 12.3 copy-start.15
  1039.4 12.9 copy-start.12
  1056.1 0.7 copy-start.2
  1056.1 0.6 copy-start.7
  1056.8 15.2 slice-start
  1059.1 12.9 slice-start.1
  1155.1 14.2 copy-start.3
  1155.1 14.2 copy-start.8
  1155.1 14.2 copy-start.9
  1155.1 16.2 copy-start.10
  1155.1 34.1 %slice-start.2 = ((s8[11534336]{0:T(1024)(128)(4,1)}), s8[4194304]{0:T(1024)(128)(4,1)S(1)}, s32[]{:S(2)}) async-start(s8[11534336]{0:T(1024)(128)(4,1)} %bitcast.109), calls=%async_computation.4 | async-start | bytes 8388608
  1155.1 34.1 %slice-start.3 = ((s8[11534336]{0:T(1024)(128)(4,1)}), s8[4194304]{0:T(1024)(128)(4,1)S(1)}, s32[]{:S(2)}) async-start(s8[11534336]{0:T(1024)(128)(4,1)} %bitcast.109), calls=%async_computation.5 | async-start | bytes 8388608
  1169.3 2.0 copy-start.18
  1171.3 18.0 %slice-start.4 = ((s8[11534336]{0:T(1024)(128)(4,1)}), s8[3145728]{0:T(1024)(128)(4,1)S(1)}, s32[]{:S(2)}) async-start(s8[11534336]{0:T(1024)(128)(4,1)} %bitcast.109), calls=%async_computation.6 | async-start | bytes 6291456
  1189.2 17.7 %copy-start.5 = (s32[1024,6]{0,1:T(8,128)S(1)}, s32[1024,6]{0,1:T(8,128)}, u32[]{:S(2)}) copy-start(s32[1024,6]{0,1:T(8,128)} %copy-done.4) | copy-start | bytes 73732
  1738.3 24.4 %copy-start.1 = (bf16[2048,64]{0,1:T(8,128)(2,1)S(1)}, bf16[2048,64]{0,1:T(8,128)(2,1)}, u32[]{:S(2)}) copy-start(bf16[2048,64]{0,1:T(8,128)(2,1)} %param.30) | copy-start | bytes 786436
where the time goes:
time: 1770 us; the launch traced here: 1760 us
  matrix products  707 us (40%)
  blocking collectives  559 us (32%)
  waiting for transfers between devices  285 us (16%)
  other arithmetic  135 us (8%)
  local copies, waits for them, and re-layouts  67.1 us (4%)
    dot_general x16, matrix products, _mm(): return jnp.einsum(form, a, b, preferred_element_type=jnp.float32)  670 us
    all_to_all x1, blocking collectives, local(): recv = lax.all_to_all(send, 'ep', 0, 0, tiled=True)  559 us
    all_to_all x1, waiting for transfers between devices, local(): back = lax.all_to_all(y, 'ep', 0, 0, tiled=True).reshape(ne * cap, d)  285 us
    reduce_or x1, other arithmetic, _route(): disp = jnp.any(hit, axis=-2).astype(jnp.bfloat16)  64.1 us
    reduce_sum x1, other arithmetic, _route(): comb = jnp.sum(jnp.where(hit, gate[..., None], 0.0), axis=-2)  58.1 us
    sub x1, matrix products, _dense(): jax.nn.softmax(jnp.where(causal, sc, -1e+30), axis=-1).astype(jnp.bfloat16)  37.2 us
  transfers between devices with their start and end apart: 1, of which 1 were waited for; matrix products, arithmetic and copies ran while one was open for 15% of the time, Pallas kernels for 0%

commit v1 on v0

v1 whole, which is shorter than its diff:
```python
import functools

import jax
import jax.numpy as jnp
from jax import lax
from jax.experimental import pallas as pl
from jax.experimental.pallas import tpu as pltpu
from jax.sharding import PartitionSpec as P

HEAD = 128
EPS = 1e-6
CAP_FACTOR = 2
LANE = 128
TM = 256
BLK = 64
PARTS = 2
CHUNKS = ((0, 1), (1, 2))
SUB = 8
VMEM = 63000 * 1024


def _mm(form, a, b):
    return jnp.einsum(form, a, b, preferred_element_type=jnp.float32)


def _rms(x, w):
    xf = x.astype(jnp.float32)
    r = lax.rsqrt(jnp.mean(xf * xf, axis=-1, keepdims=True) + EPS)
    return (xf * r * w.astype(jnp.float32)).astype(jnp.bfloat16)


def _qkv(h0, ln_attn, wq, wk, wv):
    x1 = _rms(h0, ln_attn)
    return (_mm('sd,de->se', x1, wq), _mm('sd,de->se', x1, wk), _mm('sd,de->se', x1, wv).astype(jnp.bfloat16))


def _heads(q, k, v):
    s, w = q.shape
    half, bq = HEAD // 2, min(256, s)
    freq = 10000.0 ** (-jnp.arange(half, dtype=jnp.float32) / half)
    ang = jnp.arange(s, dtype=jnp.float32)[:, None] * freq[None, :]
    c, sn = jnp.cos(ang), jnp.sin(ang)
    cos = jnp.concatenate([c, c], axis=1)
    sin = jnp.concatenate([-sn, sn], axis=1)

    def body(cos_ref, sin_ref, q_ref, k_ref, v_ref, o_ref):
        def rot(x):
            return (x * cos_ref[...] + pltpu.roll(x, half, 1) * sin_ref[...]).astype(jnp.bfloat16)

        qr, kr = rot(q_ref[...]), rot(k_ref[...])
        for i in range(s // bq):
            n = (i + 1) * bq
            sc = lax.dot_general(qr[i * bq:n], kr[:n], (((1,), (1,)), ((), ())),
                                 preferred_element_type=jnp.float32) * HEAD ** -0.5
            row = lax.broadcasted_iota(jnp.int32, (bq, n), 0) + i * bq
            col = lax.broadcasted_iota(jnp.int32, (bq, n), 1)
            sc = jnp.where(row >= col, sc, -1e30)
            ex = jnp.exp(sc - jnp.max(sc, axis=-1, keepdims=True))
            p = (ex / jnp.sum(ex, axis=-1, keepdims=True)).astype(jnp.bfloat16)
            o_ref[i * bq:n, :] = jnp.dot(p, v_ref[:n, :], preferred_element_type=jnp.float32).astype(jnp.bfloat16)

    col = pl.BlockSpec((s, HEAD), lambda h: (0, h))
    tab = pl.BlockSpec((s, HEAD), lambda h: (0, 0))
    return pl.pallas_call(
        body,
        out_shape=jax.ShapeDtypeStruct((s, w), jnp.bfloat16),
        grid=(w // HEAD,),
        in_specs=[tab, tab, col, col, col],
        out_specs=col,
        compiler_params=pltpu.CompilerParams(dimension_semantics=('arbitrary',), vmem_limit_bytes=VMEM),
        cost_estimate=pl.CostEstimate(flops=20_000_000_000, bytes_accessed=24_000_000, transcendentals=0),
        name='heads',
    )(cos, sin, q, k, v)


def _ffn(a, ln_ffn, ws1, ws3, ws2):
    x2 = _rms(a, ln_ffn)
    hs = (jax.nn.silu(_mm('sd,df->sf', x2, ws1)) * _mm('sd,df->sf', x2, ws3)).astype(jnp.bfloat16)
    return _mm('sf,fd->sd', hs, ws2)


def _gates(u, wr, idx_t):
    lg = _mm('td,de->et', u, wr)
    e = jnp.arange(wr.shape[1], dtype=idx_t.dtype)
    sel = jnp.sum(jnp.where(idx_t[:, None, :] == e[None, :, None], lg[None], 0.0), axis=1)
    return jax.nn.softmax(sel, axis=0)


def _tables(idx, gate, first, el, cap):
    _, g, tc = idx.shape
    eid = first + jnp.arange(el, dtype=jnp.int32)
    hit = idx[:, None] == eid[None, :, None, None]
    mask = jnp.any(hit, axis=0)
    w = jnp.sum(jnp.where(hit, gate[:, None], 0.0), axis=0)
    tri = (jnp.arange(tc)[:, None] <= jnp.arange(tc)[None, :]).astype(jnp.bfloat16)
    c = _mm('egt,tp->egp', mask.astype(jnp.bfloat16), tri).astype(jnp.int32)
    n = c[..., -1]
    p = jnp.arange(cap, dtype=jnp.int32)
    tok = jnp.sum((c[:, :, :, None] <= p).astype(jnp.int32), axis=2)
    ck = jnp.where(mask, c, 0)
    rowg = jnp.sum(jnp.where(ck[:, :, :, None] == p + 1, w[:, :, :, None], 0.0), axis=2)
    d = jnp.arange(g, dtype=jnp.int32)
    nt = g * tc
    lst = jnp.where(p < n[:, :, None], tok + d[None, :, None] * tc, nt).reshape(el, g * cap)
    lst = jnp.concatenate([lst, jnp.full((el, 8), nt, jnp.int32)], axis=1).reshape(-1)
    rowg = jnp.concatenate([rowg.reshape(el, g * cap), jnp.zeros((el, 8), jnp.float32)], axis=1).reshape(-1)
    ng = (n + 7) // 8
    ginc = jnp.sum(jnp.where(d[:, None] <= d[None, :], ng[:, :, None], 0), axis=1)
    gexc = ginc - ng
    gtot = ginc[:, -1]
    q = jnp.arange(g * cap // 8, dtype=jnp.int32)
    dq = jnp.sum((ginc[:, None, :] <= q[None, :, None]).astype(jnp.int32), axis=-1)
    gq = jnp.sum(jnp.where(dq[:, :, None] == d, gexc[:, None, :], 0), axis=-1)
    seg = jnp.where(q < gtot[:, None], dq * cap + (q[None] - gq) * 8, g * cap).reshape(-1)
    ntile = (gtot * 8 + TM - 1) // TM
    e = jnp.arange(el, dtype=jnp.int32)
    tinc = jnp.sum(jnp.where(e[:, None] <= e[None, :], ntile[:, None], 0), axis=0)
    texc = tinc - ntile
    total = jnp.maximum(tinc[-1], 1)
    i = jnp.minimum(jnp.arange(el * (g * cap // TM), dtype=jnp.int32), total - 1)
    te = jnp.minimum(jnp.sum((tinc[None, :] <= i[:, None]).astype(jnp.int32), axis=-1), el - 1)
    at = te[:, None] == e
    pick = lambda v: jnp.sum(jnp.where(at, v[None, :], 0), axis=-1)
    ti = jnp.where(i < tinc[-1], i - pick(texc), 0)
    live = ntile > 0
    order = jnp.sum(jnp.where(e[:, None] <= e[None, :], live[:, None].astype(jnp.int32), 0), axis=0)
    buf = pick(order) % 2
    after = jnp.min(jnp.where((e[None, :] > e[:, None]) & live[None, :], e[None, :], el), axis=-1)
    nxt = pick(after)
    return dict(lst=lst, rowg=rowg, seg=seg, gtot=gtot, te=te, ti=ti, buf=buf, nxt=nxt, total=total.reshape(1))


def _gather_rows(tb, u, el, rows):
    nt, kk, _ = u.shape
    nf = kk // SUB
    lstride, qm = rows + 8, rows // 8

    def body(te, ti, lst, seg, gtot, total, u_ref, x_ref, scr):
        i = pl.program_id(0)
        e = te[i]
        q0 = ti[i] * (TM // 8)
        ng = jnp.minimum(gtot[e] - q0, TM // 8)

        def group(z, _):
            for h in range(2):
                q = z * 2 + h
                s = seg[e * qm + q0 + q] + e * lstride
                for j in range(8):
                    v = u_ref[jnp.minimum(lst[s + j], nt - 1)].astype(jnp.float32)
                    at = pl.multiple_of((q * 8 + j) * SUB, SUB)
                    for f in range(nf):
                        scr[f, pl.ds(at, SUB), :] = v[f * SUB:(f + 1) * SUB]
            return 0

        def spread(lo, hi):
            for k in range(kk):
                x_ref[0, lo:hi, k * LANE:(k + 1) * LANE] = scr[
                    k // SUB, pl.ds(lo * SUB + k % SUB, hi - lo, stride=SUB), :].astype(jnp.bfloat16)

        @pl.when(i < total[0])
        def _():
            lax.fori_loop(0, (ng + 1) // 2, group, 0)
            spread(0, TM // 2)

            @pl.when(ng > TM // 16)
            def _():
                spread(TM // 2, TM)

    return pl.pallas_call(
        body,
        out_shape=jax.ShapeDtypeStruct((el, rows, kk * LANE), jnp.bfloat16),
        grid_spec=pltpu.PrefetchScalarGridSpec(
            num_scalar_prefetch=6, grid=(el * (rows // TM),),
            in_specs=[pl.BlockSpec(memory_space=pltpu.VMEM)],
            out_specs=pl.BlockSpec((1, TM, kk * LANE), lambda i, te, ti, *_: (te[i], ti[i], 0)),
            scratch_shapes=[pltpu.VMEM((nf, TM * SUB, LANE), jnp.float32)]),
        compiler_params=pltpu.CompilerParams(dimension_semantics=('arbitrary',), vmem_limit_bytes=VMEM),
        cost_estimate=pl.CostEstimate(flops=20_000_000_000, bytes_accessed=60_000_000, transcendentals=0),
        name='gather_rows',
    )(tb['te'], tb['ti'], tb['lst'], tb['seg'], tb['gtot'], tb['total'], u)


def _expert_rows(tb, x, ue1, ue3, ue2):
    el, rows, d = x.shape
    fe = ue1.shape[-1]
    kk = d // LANE
    nf = kk // SUB

    def body(te, ti, gtot, buf, nxt, total, x_ref, w1, w3, w2, y_ref, b1, b3, b2, sem):
        i = pl.program_id(0)
        e, b = te[i], buf[i]

        def copies(e, b):
            return [pltpu.make_async_copy(w.at[e], v.at[b], sem.at[b, k])
                    for k, (w, v) in enumerate(((w1, b1), (w3, b3), (w2, b2)))]

        @pl.when(i == 0)
        def _():
            for c in copies(e, b):
                c.start()

        @pl.when((ti[i] == 0) & (i < total[0]))
        def _():
            for c in copies(e, b):
                c.wait()

            @pl.when(nxt[i] < el)
            def _():
                for c in copies(nxt[i], 1 - b):
                    c.start()

        def compute(m):
            xv = x_ref[0, :m]
            h1 = jnp.dot(xv, b1[b], preferred_element_type=jnp.float32)
            h3 = jnp.dot(xv, b3[b], preferred_element_type=jnp.float32)
            he = (jax.nn.silu(h1) * h3).astype(jnp.bfloat16)
            y = jnp.dot(he, b2[b], preferred_element_type=jnp.float32)
            y = y.astype(jnp.bfloat16).astype(jnp.float32)
            for k in range(kk):
                y_ref[0, k // SUB, pl.ds(k % SUB, m, stride=SUB), :] = y[:, k * LANE:(k + 1) * LANE]

        left = gtot[e] * 8 - ti[i] * TM

        @pl.when((i < total[0]) & (left > TM // 2))
        def _():
            compute(TM)

        @pl.when((i < total[0]) & (left <= TM // 2))
        def _():
            compute(TM // 2)

    return pl.pallas_call(
        body,
        out_shape=jax.ShapeDtypeStruct((el, nf, rows * SUB, LANE), jnp.float32),
        grid_spec=pltpu.PrefetchScalarGridSpec(
            num_scalar_prefetch=6, grid=(el * (rows // TM),),
            in_specs=[pl.BlockSpec((1, TM, d), lambda i, te, ti, *_: (te[i], ti[i], 0))]
            + [pl.BlockSpec(memory_space=pl.ANY)] * 3,
            out_specs=pl.BlockSpec((1, nf, TM * SUB, LANE), lambda i, te, ti, *_: (te[i], 0, ti[i], 0)),
            scratch_shapes=[pltpu.VMEM((2, d, fe), jnp.bfloat16), pltpu.VMEM((2, d, fe), jnp.bfloat16),
                            pltpu.VMEM((2, fe, d), jnp.bfloat16), pltpu.SemaphoreType.DMA((2, 3))]),
        compiler_params=pltpu.CompilerParams(dimension_semantics=('arbitrary',), vmem_limit_bytes=VMEM),
        cost_estimate=pl.CostEstimate(flops=110_000_000_000, bytes_accessed=200_000_000, transcendentals=0),
        name='expert_rows',
    )(tb['te'], tb['ti'], tb['gtot'], tb['buf'], tb['nxt'], tb['total'], x, ue1, ue3, ue2)


def _combine_rows(tb, y, nt, kk):
    el = y.shape[0]
    nf = kk // SUB
    rows = y.shape[2] // SUB
    lstride, qm = rows + 8, rows // 8
    zb = 64

    def body(te, ti, lst, rowg, seg, gtot, total, y_ref, m_ref, acc, sem):
        i = pl.program_id(0)
        e = te[i]
        q0 = ti[i] * (TM // 8)
        ng = jnp.minimum(gtot[e] - q0, TM // 8)

        @pl.when(i == 0)
        def _():
            def zero(z, _):
                acc[pl.ds(pl.multiple_of(z * zb, zb), zb)] = jnp.zeros((zb, kk, LANE), jnp.float32)
                return 0
            lax.fori_loop(0, nt // zb, zero, 0)

        def group(z, _):
            toks, new = [], []
            for h in range(2):
                q = z * 2 + h
                s = seg[e * qm + q0 + q] + e * lstride
                for j in range(8):
                    at = pl.multiple_of((q * 8 + j) * SUB, SUB)
                    t, g = lst[s + j], rowg[s + j]
                    toks.append(t)
                    new.append([acc[t, f * SUB:(f + 1) * SUB] + g * y_ref[0, f, pl.ds(at, SUB), :] for f in range(nf)])
            for t, v in zip(toks, new):
                for f in range(nf):
                    acc[t, f * SUB:(f + 1) * SUB] = v[f]
            return 0

        @pl.when(i < total[0])
        def _():
            lax.fori_loop(0, (ng + 1) // 2, group, 0)

        @pl.when(i == pl.num_programs(0) - 1)
        def _():
            c = pltpu.make_async_copy(acc.at[pl.ds(0, nt)], m_ref, sem)
            c.start()
            c.wait()

    return pl.pallas_call(
        body,
        out_shape=jax.ShapeDtypeStruct((nt, kk, LANE), jnp.float32),
        grid_spec=pltpu.PrefetchScalarGridSpec(
            num_scalar_prefetch=7, grid=(el * (rows // TM),),
            in_specs=[pl.BlockSpec((1, nf, TM * SUB, LANE), lambda i, te, ti, *_: (te[i], 0, ti[i], 0))],
            out_specs=pl.BlockSpec(memory_space=pl.ANY),
            scratch_shapes=[pltpu.VMEM((nt + 8, kk, LANE), jnp.float32), pltpu.SemaphoreType.DMA]),
        compiler_params=pltpu.CompilerParams(dimension_semantics=('arbitrary',), vmem_limit_bytes=VMEM),
        cost_estimate=pl.CostEstimate(flops=20_000_000_000, bytes_accessed=100_000_000, transcendentals=0),
        name='combine_rows',
    )(tb['te'], tb['ti'], tb['lst'], tb['rowg'], tb['seg'], tb['gtot'], tb['total'], y)


def solution(mesh):
    g_ = mesh.shape['ep']
    rows = P(('dp', 'ep'))
    rep = P()

    def local(h0, idx, slot, ln_attn, wq, wk, wv, wo, ln_ffn, ws1, ws3, ws2, ln_moe, wr, ue1, ue3, ue2):
        b, s, d = h0.shape
        top = idx.shape[-1]
        el = ue1.shape[0]
        ne = el * g_
        t = b * s
        kk = d // LANE
        cap = CAP_FACTOR * t * top // ne
        nb = t // (BLK * PARTS)
        first = lax.axis_index('ep').astype(jnp.int32) * el

        u = _rms(h0, ln_moe).reshape(t, d)
        u4 = u.reshape(nb, PARTS, BLK, kk, LANE)
        us = []
        for lo, hi in CHUNKS:
            tc = nb * (hi - lo) * BLK
            us.append(lax.all_gather(u4[:, lo:hi].reshape(tc, kk, LANE), 'ep', axis=0))
        idx_t = idx.reshape(t, top).T
        gate = _gates(u, wr, idx_t)
        meta = lax.all_gather(jnp.concatenate([idx_t.astype(jnp.float32), gate], axis=0), 'ep', axis=1)
        meta = meta.reshape(2 * top, g_, nb, PARTS, BLK)
        tables = []
        for lo, hi in CHUNKS:
            mc = meta[:, :, :, lo:hi].reshape(2 * top, g_, -1)
            tables.append(_tables(mc[:top].astype(jnp.int32), mc[top:], first, el, cap))

        hd = h0.reshape(t, d)
        q, k, v = _qkv(hd, ln_attn, wq, wk, wv)
        q, k, v, us[0] = lax.optimization_barrier((q, k, v, us[0]))
        ms = []
        for c, (lo, hi) in enumerate(CHUNKS):
            uc, tb = us[c], tables[c]
            nt = uc.shape[0] * uc.shape[1]
            x = _gather_rows(tb, uc.reshape(nt, kk, LANE), el, g_ * cap)
            y = _expert_rows(tb, x, ue1, ue3, ue2)
            m = _combine_rows(tb, y, nt, kk)
            if c == len(CHUNKS) - 1:
                q, k, v, m = lax.optimization_barrier((q, k, v, m))
            else:
                us[c + 1], m = lax.optimization_barrier((us[c + 1], m))
            m = lax.psum_scatter(m, 'ep', scatter_dimension=0, tiled=True)
            ms.append(m.reshape(nb, hi - lo, BLK, kk, LANE))
        o = jnp.concatenate([_heads(*(z[n * s:(n + 1) * s] for z in (q, k, v))) for n in range(b)], axis=0)
        a = (hd.astype(jnp.float32) + _mm('se,ed->sd', o, wo)).astype(jnp.bfloat16)
        fo = _ffn(a, ln_ffn, ws1, ws3, ws2)
        m = jnp.concatenate(ms, axis=1).reshape(t, d)
        out = a.astype(jnp.float32) + fo + m
        return out.astype(jnp.bfloat16).reshape(b, s, d)

    specs = (rows, rows, rows) + (rep,) * 11 + (P('ep'), P('ep'), P('ep'))
    return jax.shard_map(local, mesh=mesh, in_specs=specs, out_specs=rows, check_vma=False)
```

time: 1770 us -> 751 us (0.42)
  matrix products: 707 us -> 112 us
  blocking collectives: 559 us -> 27.3 us
  Pallas kernels: 0 us -> 474 us
  waiting for transfers between devices: 285 us -> 69.1 us
  other arithmetic: 135 us -> 40.5 us
  local copies, waits for them, and re-layouts: 67.1 us -> 17.1 us
    all_to_all x1 -> x0, blocking collectives: 559 us -> none  [local(): recv = lax.all_to_all(send, 'ep', 0, 0, tiled=True)]
    dot_general x16 -> x10, matrix products: 670 us -> 112 us  [_mm(): return jnp.einsum(form, a, b, preferred_element_type=jnp.float32)]
    pallas_call x0 -> x7, Pallas kernels: none -> 474 us  [the longest x2 271 us: _expert_rows(): pl.pallas_call(body, out_shape=jax.ShapeDtypeStruct((el, nf, rows * SUB,...]
    all_to_all x1 -> x0, waiting for transfers between devices: 285 us -> none  [local(): back = lax.all_to_all(y, 'ep', 0, 0, tiled=True).reshape(ne * cap, d)]
    reduce_scatter x0 -> x2, waiting for transfers between devices: none -> 68.2 us  [local(): m = lax.psum_scatter(m, 'ep', scatter_dimension=0, tiled=True)]
    reduce_or x1, other arithmetic: 64.1 us -> 0.25 us  [_tables(): mask = jnp.any(hit, axis=0)]
    reduce_sum x3 -> x18, other arithmetic: 58.9 us -> 14.5 us  [the longest x1 6.25 us: _tables(): jnp.sum(jnp.where(ck[:, :, :, None] == p + 1, w[:, :, :, None], 0.0), axi...]
    sub x1 -> x0, matrix products: 37.2 us -> none  [_dense(): jax.nn.softmax(jnp.where(causal, sc, -1e+30), axis=-1).astype(jnp.bfloat16)]
  transfers between devices with their start and end apart: 1 -> 4, of which waited for: 1 -> 1; matrix products, arithmetic and copies ran while one was open for 15% -> 17% of each run, Pallas kernels for 0% -> 63%
where the time goes in v1:
time: 751 us; the launch traced here: 755 us
  Pallas kernels  474 us (63%)
  matrix products  112 us (15%)
  waiting for transfers between devices  69.1 us (9%)
  other arithmetic  40.5 us (5%)
  blocking collectives  27.3 us (4%)
  local copies, waits for them, and re-layouts  17.1 us (2%)
  between operations  15.2 us (2%)
    pallas_call x2, Pallas kernels, _expert_rows(): pl.pallas_call(body, out_shape=jax.ShapeDtypeStruct((el, nf, rows * SUB,...  271 us
    dot_general x10, matrix products, _mm(): return jnp.einsum(form, a, b, preferred_element_type=jnp.float32)  112 us
    pallas_call x2, Pallas kernels, _combine_rows(): pl.pallas_call(body, out_shape=jax.ShapeDtypeStruct((nt, kk, LANE), jnp.f...  92.9 us
    pallas_call x2, Pallas kernels, _gather_rows(): pl.pallas_call(body, out_shape=jax.ShapeDtypeStruct((el, rows, kk * LANE)...  69.6 us
    reduce_scatter x2, waiting for transfers between devices, local(): m = lax.psum_scatter(m, 'ep', scatter_dimension=0, tiled=True)  68.2 us
    pallas_call x1, Pallas kernels, _heads(): pl.pallas_call(body, out_shape=jax.ShapeDtypeStruct((s, w), jnp.bfloat16)...  40.5 us
    all_gather x1, blocking collectives, local(): lax.all_gather(jnp.concatenate([idx_t.astype(jnp.float32), gate], axis=0)...  27.3 us
  transfers between devices with their start and end apart: 4, of which 1 were waited for; matrix products, arithmetic and copies ran while one was open for 17% of the time, Pallas kernels for 63%

profile of v1, /device:TPU:112, one launch (start us, length us, event | category | flops | bytes accessed | tf_op | source)
XLA Modules:
  0.0 754.7 jit_solution(10395998915079591859)
XLA Ops:
  6.6 3.1 fusion.12
  10.4 3.3 fusion.22
  13.7 1.4 copy.22
  15.2 2.7 fusion.68
  19.0 3.6 fusion.23
  23.0 27.3 %all-gather = f32[12,8192]{1,0:T(8,128)S(1)} all-gather(f32[12,1024]{1,0:T(8,128)S(1)} %pad_maximum_fusion.3), channel_id=2, replica_groups=mesh['dp'=2,'ep'=8] {'ep'}, dimensions={1}, use_global_device_ids=true | all-gather | bytes 442368 | tf_op jit(solution)/shard_map/all_gather | solution.py:331
  50.9 1.2 fusion.34
  54.1 2.7 convert_reduce_fusion
  58.0 6.2 select_reduce_fusion
  65.0 2.7 convert_reduce_fusion.1
  74.0 1.2 compare_select_fusion.6.ti
  75.7 3.2 fusion.8
  79.6 14.0 %convolution_convert_fusion.v_ref = bf16[1024,2048]{1,0:T(8,128)(2,1)} fusion(bf16[2048,2048]{1,0:T(8,128)(2,1)} %param.22, bf16[1,1024,2048]{2,1,0:T(8,128)(2,1)} %param.17, f32[2048]{0:T(1024)S(1)} %convert_element_type.103, f32[1024]{0:T(1024)S(1)} %add_rsqrt_fusion.2), kind=kOutput, calls=%fused_computation.32 | convolution fusion | flops 8600420352 | bytes 16789504 | tf_op jit(solution)/shard_map/sd,de->se/dot_general | solution.py:23
  93.7 11.4 %fusion.62.k_ref = f32[1024,2048]{1,0:T(8,128)} fusion(bf16[2048,2048]{1,0:T(8,128)(2,1)S(1)} %bitcast.94, bf16[1,1024,2048]{2,1,0:T(8,128)(2,1)S(1)} %copy-done.2, f32[2048]{0:T(1024)S(1)} %convert_element_type.103, f32[1024]{0:T(1024)S(1)} %add_rsqrt_fusion.2), kind=kOutput, calls=%fused_computation.191 | convolution fusion | flops 8598323200 | bytes 20983808 | tf_op jit(solution)/shard_map/sd,de->se/dot_general | solution.py:23
  105.1 11.3 %fusion.64.q_ref = f32[1024,2048]{1,0:T(8,128)} fusion(bf16[2048,2048]{1,0:T(8,128)(2,1)S(1)} %bitcast.96, bf16[1,1024,2048]{2,1,0:T(8,128)(2,1)S(1)} %copy-done.2, f32[2048]{0:T(1024)S(1)} %convert_element_type.103, f32[1024]{0:T(1024)S(1)} %add_rsqrt_fusion.2), kind=kOutput, calls=%fused_computation.192 | convolution fusion | flops 8598323200 | bytes 20983808 | tf_op jit(solution)/shard_map/sd,de->se/dot_general | solution.py:23
  116.4 35.9 %gather_rows.2.x_ref = bf16[8,1536,2048]{2,1,0:T(8,128)(2,1)} custom-call(s32[48]{0:T(128)} %copy-done.11, s32[48]{0:T(128)} %compare_select_fusion.6.ti, s32[12352]{0:T(1024)} %reshape.300.lst, s32[1536]{0:T(1024)} %get-tuple-element.63.seg, s32[8]{0:T(128)} %copy-done.8, s32[1]{0:T(128)} %bitcast.10.total, bf16[4096,16,128]{2,1,0:T(8,128)(2,1)} %bitcast.90), custom_call_target="tpu_custom_call" | custom-call | flops 20000000000 | bytes 60000000 | tf_op jit(solution)/shard_map/gather_rows/pallas_call | solution.py:169
  152.3 140.7 %expert_rows.2.y_ref = f32[8,2,12288,128]{3,2,1,0:T(8,128)} custom-call(s32[48]{0:T(128)} %copy-done.11, s32[48]{0:T(128)} %compare_select_fusion.6.ti, s32[8]{0:T(128)} %copy-done.8, s32[48]{0:T(128)} %and_select_fusion.buf, s32[48]{0:T(128)} %get-tuple-element.43.nxt, s32[1]{0:T(128)} %bitcast.10.total, bf16[8,1536,2048]{2,1,0:T(8,128)(2,1)} %gather_rows.2.x_ref, ...), custom_call_target="tpu_custom_call" | custom-call | flops 109999996928 | bytes 200000000 | tf_op jit(solution)/shard_map/expert_rows/pallas_call | solution.py:232
  293.0 47.8 %combine_rows.2 = f32[4096,16,128]{2,1,0:T(8,128)} custom-call(s32[48]{0:T(128)} %copy-done.11, s32[48]{0:T(128)} %compare_select_fusion.6.ti, s32[12352]{0:T(1024)} %reshape.300.lst, f32[12352]{0:T(1024)} %reshape.302.rowg, s32[1536]{0:T(1024)} %get-tuple-element.63.seg, s32[8]{0:T(128)} %copy-done.8, s32[1]{0:T(128)} %bitcast.10.total, ...), custom_call_target="tpu_custom_call" | custom-call | flops 20000000000 | bytes 100000000 | tf_op jit(solution)/shard_map/combine_rows/pallas_call | solution.py:293
  347.2 33.7 %gather_rows.3.x_ref = bf16[8,1536,2048]{2,1,0:T(8,128)(2,1)} custom-call(s32[48]{0:T(128)} %copy-done.12, s32[48]{0:T(128)} %compare_select_fusion.7.ti, s32[12352]{0:T(1024)} %reshape.296.lst, s32[1536]{0:T(1024)} %get-tuple-element.64.seg, s32[8]{0:T(128)} %copy-done.6, s32[1]{0:T(128)} %bitcast.7.total, bf16[4096,16,128]{2,1,0:T(8,128)(2,1)} %bitcast.89), custom_call_target="tpu_custom_call" | custom-call | flops 20000000000 | bytes 60000000 | tf_op jit(solution)/shard_map/gather_rows/pallas_call | solution.py:169
  380.9 129.9 %expert_rows.3.y_ref = f32[8,2,12288,128]{3,2,1,0:T(8,128)} custom-call(s32[48]{0:T(128)} %copy-done.12, s32[48]{0:T(128)} %compare_select_fusion.7.ti, s32[8]{0:T(128)} %copy-done.6, s32[48]{0:T(128)} %and_select_fusion.2.buf, s32[48]{0:T(128)} %get-tuple-element.50.nxt, s32[1]{0:T(128)} %bitcast.7.total, bf16[8,1536,2048]{2,1,0:T(8,128)(2,1)} %gather_rows.3.x_ref, ...), custom_call_target="tpu_custom_call" | custom-call | flops 109999996928 | bytes 200000000 | tf_op jit(solution)/shard_map/expert_rows/pallas_call | solution.py:232
  510.9 45.1 %combine_rows.3 = f32[4096,16,128]{2,1,0:T(8,128)} custom-call(s32[48]{0:T(128)} %copy-done.12, s32[48]{0:T(128)} %compare_select_fusion.7.ti, s32[12352]{0:T(1024)} %reshape.296.lst, f32[12352]{0:T(1024)} %reshape.298.rowg, s32[1536]{0:T(1024)} %get-tuple-element.64.seg, s32[8]{0:T(128)} %copy-done.6, s32[1]{0:T(128)} %bitcast.7.total, ...), custom_call_target="tpu_custom_call" | custom-call | flops 20000000000 | bytes 100000000 | tf_op jit(solution)/shard_map/combine_rows/pallas_call | solution.py:293
  556.7 2.0 fusion.33
  558.6 1.3 pad_maximum_fusion.1
  560.0 40.5 %heads.1 = bf16[1024,2048]{1,0:T(8,128)(2,1)} custom-call(f32[1024,128]{1,0:T(8,128)} %get-tuple-element.81.cos_ref, f32[1024,128]{1,0:T(8,128)} %get-tuple-element.82.sin_ref, f32[1024,2048]{1,0:T(8,128)} %fusion.64.q_ref, f32[1024,2048]{1,0:T(8,128)} %fusion.62.k_ref, bf16[1024,2048]{1,0:T(8,128)(2,1)} %convolution_convert_fusion.v_ref), custom_call_target="tpu_custom_call" | custom-call | flops 20000000000 | bytes 24000000 | tf_op jit(solution)/shard_map/heads/pallas_call | solution.py:64
  600.5 13.7 %fusion.3 = (f32[1024]{0:T(1024)S(1)}, bf16[1024,2048]{1,0:T(8,128)(2,1)S(1)}) fusion(bf16[1024,2048]{1,0:T(8,128)(2,1)} %heads.1, bf16[2048,2048]{1,0:T(8,128)(2,1)} %param.23, bf16[1,1024,2048]{2,1,0:T(8,128)(2,1)} %param.17), kind=kOutput, calls=%fused_computation.16 | convolution fusion | flops 8602516480 | bytes 20975616 | tf_op jit(solution)/shard_map/se,ed->sd/dot_general | solution.py:23
  614.3 2.0 copy-done.15
  616.3 17.8 %fusion.19 = f32[1024,2816]{1,0:T(8,128)} fusion(bf16[2048,2816]{1,0:T(8,128)(2,1)} %param.25, bf16[1024,2048]{1,0:T(8,128)(2,1)S(1)} %get-tuple-element.73, f32[2048]{0:T(1024)S(1)} %convert_element_type.124, f32[1024]{0:T(1024)S(1)} %add_rsqrt_fusion), kind=kOutput, calls=%fused_computation.35 | convolution fusion | flops 11819548672 | bytes 27275264 | tf_op jit(solution)/shard_map/sd,df->sf/dot_general | solution.py:23
  634.1 17.7 %multiply_convert_fusion = bf16[1024,2816]{1,0:T(8,128)(2,1)} fusion(f32[1024,2816]{1,0:T(8,128)} %fusion.19, bf16[2048,2816]{1,0:T(8,128)(2,1)S(1)} %bitcast.92, bf16[1024,2048]{1,0:T(8,128)(2,1)} %copy-done.15, f32[2048]{0:T(1024)S(1)} %convert_element_type.124, f32[1024]{0:T(1024)S(1)} %add_rsqrt_fusion), kind=kOutput, calls=%fused_computation.15 | convolution fusion | flops 11836850176 | bytes 33042432 | tf_op jit(solution)/shard_map/sd,df->sf/dot_general | solution.py:23
  651.8 68.2 %reduce-scatter.5.cloned.1.call-done = f32[512,16,128]{2,1,0:T(8,128)} async-done(((f32[4096,16,128]{2,1,0:T(8,128)}), f32[512,16,128]{2,1,0:T(8,128)}) %reduce-scatter.5.cloned.1.call-update) | async-done | bytes 4194320 | tf_op jit(solution)/shard_map/reduce_scatter | solution.py:352
  720.0 4.0 pad_maximum_fusion
  724.8 1.4 copy-done.16
  726.2 21.8 %fusion.15 = bf16[1,1024,2048]{2,1,0:T(8,128)(2,1)} fusion(f32[128,8,16,128]{3,2,1,0:T(8,128)S(1)} %bitcast.84, bf16[1024,2048]{1,0:T(8,128)(2,1)S(1)} %copy-done.16, bf16[1024,2816]{1,0:T(8,128)(2,1)} %multiply_convert_fusion, bf16[2816,2048]{1,0:T(8,128)(2,1)} %param.27), kind=kOutput, calls=%fused_computation.29 | convolution fusion | flops 11819548672 | bytes 34078720 | tf_op jit(solution)/shard_map/sf,fd->sd/dot_general | solution.py:23
  (151 shorter events, 20.4 us)
Async XLA Ops:
  6.5 12.5 %copy-start = (bf16[2048,64]{0,1:T(8,128)(2,1)S(1)}, bf16[2048,64]{0,1:T(8,128)(2,1)}, u32[]{:S(2)}) copy-start(bf16[2048,64]{0,1:T(8,128)(2,1)} %param.29) | copy-start | bytes 786436
  6.6 109.8 %all-gather.4.cloned.1.call-start = ((), (), s32[]{:S(2)}) async-start(), calls=%async_computation.2 | async-start | bytes 18874368 | tf_op jit(solution)/shard_map/all_gather | solution.py:328
  15.1 3.8 copy-start.9
  15.1 3.9 copy-start.5
  17.9 323.0 %all-gather.6.cloned.1.call-start = ((), (), s32[]{:S(2)}) async-start(), calls=%async_computation.3 | async-start | bytes 18874368 | tf_op jit(solution)/shard_map/all_gather | solution.py:328
  18.7 633.1 %reduce-scatter.3.cloned.1.call-start = ((), (), s32[]{:S(2)}) async-start(), calls=%async_computation.4 | async-start | bytes 37748736 | tf_op jit(solution)/shard_map/reduce_scatter | solution.py:352
  69.2 0.9 copy-start.6
  69.2 24.4 %copy-start.8 = (s32[8]{0:T(128)}, s32[8]{0:T(128)S(1)}, u32[]{:S(2)}) copy-start(s32[8]{0:T(128)S(1)} %get-tuple-element.34.gtot) | copy-start | bytes 100
  73.3 20.3 %copy-start.11 = (s32[48]{0:T(128)}, s32[48]{0:T(128)S(1)}, u32[]{:S(2)}) copy-start(s32[48]{0:T(128)S(1)} %broadcast_minimum_fusion.te) | copy-start | bytes 580
  75.7 17.9 %slice-start.3 = ((s8[8388608]{0:T(1024)(128)(4,1)}), s8[4194304]{0:T(1024)(128)(4,1)S(1)}, s32[]{:S(2)}) async-start(s8[8388608]{0:T(1024)(128)(4,1)} %bitcast.93), calls=%async_computation.9 | async-start | bytes 8388608
  79.6 14.0 %copy-start.2 = (bf16[1,1024,2048]{2,1,0:T(8,128)(2,1)S(1)}, bf16[1,1024,2048]{2,1,0:T(8,128)(2,1)}, u32[]{:S(2)}) copy-start(bf16[1,1024,2048]{2,1,0:T(8,128)(2,1)} %param.17) | copy-start | bytes 12582916
  79.6 14.1 %slice-start.4 = ((s8[8388608]{0:T(1024)(128)(4,1)}), s8[4194304]{0:T(1024)(128)(4,1)S(1)}, s32[]{:S(2)}) async-start(s8[8388608]{0:T(1024)(128)(4,1)} %bitcast.93), calls=%async_computation.10 | async-start | bytes 8388608
  79.6 25.5 %slice-start.5 = ((s8[8388608]{0:T(1024)(128)(4,1)}), s8[4194304]{0:T(1024)(128)(4,1)S(1)}, s32[]{:S(2)}) async-start(s8[8388608]{0:T(1024)(128)(4,1)} %bitcast.95), calls=%async_computation.11 | async-start | bytes 8388608
  93.7 11.4 %slice-start.6 = ((s8[8388608]{0:T(1024)(128)(4,1)}), s8[4194304]{0:T(1024)(128)(4,1)S(1)}, s32[]{:S(2)}) async-start(s8[8388608]{0:T(1024)(128)(4,1)} %bitcast.95), calls=%async_computation.12 | async-start | bytes 8388608
  340.8 0.7 copy-start.14
  340.8 2.1 copy-start.3
  340.8 2.9 copy-start.4
  340.8 3.6 copy-start.7
  340.8 3.8 copy-start.13
  340.9 379.0 %reduce-scatter.5.cloned.1.call-start = ((), (), s32[]{:S(2)}) async-start(), calls=%async_computation.5 | async-start | bytes 37748736 | tf_op jit(solution)/shard_map/reduce_scatter | solution.py:352
  344.8 2.5 copy-start.12
  556.0 0.7 copy-start.10
  600.5 33.5 %slice-start = ((s8[11534336]{0:T(1024)(128)(4,1)}), s8[4194304]{0:T(1024)(128)(4,1)S(1)}, s32[]{:S(2)}) async-start(s8[11534336]{0:T(1024)(128)(4,1)} %bitcast.91), calls=%async_computation.6 | async-start | bytes 8388608
  600.5 33.5 %slice-start.1 = ((s8[11534336]{0:T(1024)(128)(4,1)}), s8[4194304]{0:T(1024)(128)(4,1)S(1)}, s32[]{:S(2)}) async-start(s8[11534336]{0:T(1024)(128)(4,1)} %bitcast.91), calls=%async_computation.7 | async-start | bytes 8388608
  614.3 2.0 copy-start.15
  616.3 17.8 %slice-start.2 = ((s8[11534336]{0:T(1024)(128)(4,1)}), s8[3145728]{0:T(1024)(128)(4,1)S(1)}, s32[]{:S(2)}) async-start(s8[11534336]{0:T(1024)(128)(4,1)} %bitcast.91), calls=%async_computation.8 | async-start | bytes 6291456
  724.0 2.2 copy-start.16
  726.2 21.8 %copy-start.1 = (bf16[2048,64]{0,1:T(8,128)(2,1)S(1)}, bf16[2048,64]{0,1:T(8,128)(2,1)}, u32[]{:S(2)}) copy-start(bf16[2048,64]{0,1:T(8,128)(2,1)} %param.29) | copy-start | bytes 786436
Sparse Core Ops, SparseCore 0:
  18.0 86.7 all-gather.3
  106.4 81.6 all-gather.5
  341.1 163.7 reduce-scatter.2
  556.2 163.7 reduce-scatter.4
